TPU v7x, 32 devices: a whole 2x2x4 slice. The times are simulated.
32 devices in a mesh: groups: 2 (over x), ctx: 16 (over z, y, core).
Axes of the slice: x: 2, y: 2, z: 4, core: 2. Of those that a mesh axis runs over, the one named last changes fastest.
Arguments:
- queries: bfloat16 [3072, 16, 128], P(('groups', 'ctx')), parts along dimension 0, may hold values from -12 to 12
- keys: bfloat16 [3072, 4, 128], P(('groups', 'ctx')), parts along dimension 0, may hold values from -5 to 5
- values: bfloat16 [3072, 4, 128], P(('groups', 'ctx')), parts along dimension 0, may hold values from -6 to 6
- positions: int32 [3072], P(('groups', 'ctx')), parts along dimension 0, may hold values from 0 to 1535, as said below
Outputs:
- attended: bfloat16 [3072, 16, 128], P(('groups', 'ctx')), parts along dimension 0
There are 2 independent parts, one for each index of `groups`. A program takes and returns all parts, laid end to end along the dimension named above; each array names one. Nothing has to cross between parts.
Inputs may be any that keep to these rules, and one draw needn't show every extreme that they name: A permutation of 0 to 1535 in which the 96 rows of each device along ctx hold the positions c, c + 16, c + 32 and so on in that order, for one offset c a device, the offsets of the devices being a permutation of 0 to 15.
All inputs are finite; a program needn't handle non-finite values.
Results may differ from a plain program's by a relative error of at most 0.0091.
Values may be sent and summed in bfloat16 or wider, within the bound.
A program may use at most 64 MiB of HBM per device.

v0:
```python
import functools
import math

import jax
import jax.numpy as jnp
import numpy as np
from jax import lax
from jax.experimental import pallas as pl
from jax.experimental.pallas import tpu as pltpu
from jax.sharding import PartitionSpec as P

UNIT = 16
PIECES = 2
PLANE = 4


def rotary_tables(tokens, head_size, stride):
    half = head_size // 2
    inverse = 1000000.0 ** (-2.0 * np.arange(half) / head_size)
    angles = (stride * np.arange(tokens))[:, None] * inverse[None, :]
    wide = lambda x: np.concatenate([x, x], -1)
    return np.concatenate(
        [wide(np.cos(angles)), wide(np.sin(angles)), wide(np.tile(inverse, (8, 1)))]
    ).astype(np.float32)


def attend(
    n, kv_heads, per_group, tokens,
    place_hbm, q_hbm, k_hbm, v_hbm, table_hbm, out_ref,
    gathered, q_rot, wide, small, m_ref, l_ref, acc_ref,
    place_ref, q_ref, k_ref, v_ref, table_ref,
    recv_sem, send_sem, load_sem,
):
    loads = [
        pltpu.make_async_copy(src, dst, load_sem.at[i])
        for i, (src, dst) in enumerate(
            [(place_hbm, place_ref), (table_hbm, table_ref), (k_hbm, k_ref), (v_hbm, v_ref), (q_hbm, q_ref)]
        )
    ]
    for load in loads[:4]:
        load.start()
    head_size = q_ref.shape[-1]
    heads = kv_heads * per_group
    rows = n // PLANE
    me = lax.axis_index("ctx")
    core = me % 2
    column = me // 2 % 2
    z = me // PLANE
    units = tokens // UNIT
    tile = 2 * UNIT
    tiles = tokens // tile
    per_piece = kv_heads // PIECES
    lanes = per_group * tile
    factor = math.log2(math.e) / math.sqrt(head_size)

    def device(row, col, cr):
        return row * PLANE + col * 2 + cr

    barrier = pltpu.get_barrier_semaphore()
    across = device(z, 1 - column, core)
    mate = device(z, column, 1 - core)
    below = me - PLANE
    above = me + PLANE

    def greet(target):
        pl.semaphore_signal(barrier, inc=1, device_id={"ctx": target})

    greet(across)
    greet(mate)

    @pl.when(z > 0)
    def _():
        greet(below)

    @pl.when(z < rows - 1)
    def _():
        greet(above)

    for load in loads[:2]:
        load.wait()
    offset = place_ref[0].astype(jnp.float32)
    start = table_ref[2 * tokens : 2 * tokens + 8, :] * offset
    c0, s0 = jnp.cos(start)[:1], jnp.sin(start)[:1]
    ct, st = table_ref[:tokens, :], table_ref[tokens : 2 * tokens, :]
    lane = lax.broadcasted_iota(jnp.int32, (tokens, head_size), 1)
    cosine = ct * c0 - st * s0
    sine = st * c0 + ct * s0
    sine = jnp.where(lane < head_size // 2, -sine, sine)

    def rotated(x):
        return (x * cosine + pltpu.roll(x, head_size // 2, 1) * sine).astype(jnp.bfloat16)

    for load in loads[2:4]:
        load.wait()
    loads[4].start()
    small[0] = k_ref[...].astype(jnp.float32)
    small[1] = v_ref[...].astype(jnp.float32)
    for h in range(kv_heads):
        at = 1 + h * 2 * units
        k = rotated(small[0, pl.ds(h, tokens, stride=kv_heads), :])
        gathered[me, at : at + units] = k.reshape(units, UNIT, head_size)
        v = small[1, pl.ds(h, tokens, stride=kv_heads), :].astype(jnp.bfloat16)
        gathered[me, at + units : at + 2 * units] = v.reshape(units, UNIT, head_size)
    own = jnp.full((UNIT, head_size), offset, jnp.float32)
    gathered[me, 0] = own.astype(jnp.bfloat16)

    def copy(slot, p, target, kind):
        blocks = 2 * units * per_piece
        first = 1 + p * blocks if p else 0
        part = gathered.at[slot, pl.ds(first, 1 + (p + 1) * blocks - first)]
        return pltpu.make_async_remote_copy(
            src_ref=part,
            dst_ref=part,
            send_sem=send_sem.at[kind, slot, p],
            recv_sem=recv_sem.at[slot, p],
            device_id={"ctx": target},
        )

    def arrived(slot, p):
        copy(slot, p, mate, 0).wait_recv()

    def share(slot, p):
        copy(slot, p, across, 1).start()
        copy(slot, p, mate, 2).start()

    pl.semaphore_wait(barrier, 2 + (z > 0).astype(jnp.int32) + (z < rows - 1).astype(jnp.int32))

    for p in range(PIECES):

        @pl.when(z > 0)
        def _():
            copy(me, p, below, 0).start()

        @pl.when(z < rows - 1)
        def _():
            copy(me, p, above, 3).start()

        share(me, p)

    loads[4].wait()
    wide[...] = q_ref[...].astype(jnp.float32)
    for h in range(heads):
        k, g = divmod(h, per_group)
        q = rotated(wide[pl.ds(h, tokens, stride=heads), :])
        for t in range(tiles):
            q_rot[k, t * lanes + g * tile : t * lanes + (g + 1) * tile] = q[t * tile : (t + 1) * tile]

    width = tiles * lanes
    m_ref[...] = jnp.full(m_ref.shape, -jnp.inf, jnp.float32)
    l_ref[...] = jnp.zeros(l_ref.shape, jnp.float32)
    acc_ref[...] = jnp.zeros(acc_ref.shape, jnp.float32)

    keys_tile = PLANE * tile
    key_row = lax.broadcasted_iota(jnp.int32, (keys_tile, lanes), 0)
    key_at = key_row % tile
    query_at = lax.broadcasted_iota(jnp.int32, (keys_tile, lanes), 1) % tile

    def attend_plane(row):
        first = row * PLANE

        def head(k):
            at = 1 + k * 2 * units
            theirs = gathered[pl.ds(first, PLANE), 0].astype(jnp.float32)
            theirs = jnp.concatenate([theirs[:, None]] * (tile // UNIT), 1)
            theirs = theirs.reshape(keys_tile, head_size)
            reach = key_at + (theirs > offset).astype(jnp.int32)
            allowed = reach <= query_at
            scores = []
            for t in range(tiles):
                keys = gathered[pl.ds(first, PLANE), pl.ds(at + 2 * t, 2)]
                keys = keys.reshape(keys_tile, head_size)
                s = lax.dot_general(
                    keys, q_rot[k, t * lanes :],
                    (((1,), (1,)), ((), ())), preferred_element_type=jnp.float32,
                )
                diagonal = jnp.where(allowed, s[:, :lanes], -jnp.inf)
                scores.append([diagonal] + [s[:, i * lanes : (i + 1) * lanes] for i in range(1, tiles - t)])
            old = m_ref[k]
            weights = [[] for _ in range(tiles)]
            shrinks = []
            for i in range(tiles):
                span = slice(i * lanes, (i + 1) * lanes)
                mine = [scores[t][i - t] for t in range(i + 1)]
                top = old[:, span]
                for s in mine:
                    top = jnp.maximum(top, jnp.max(s, axis=0, keepdims=True))
                shrink = jnp.exp2((old[:, span] - top) * factor)
                total = l_ref[k, :, span] * shrink
                for t in range(i + 1):
                    w = jnp.exp2((mine[t] - top) * factor)
                    total += jnp.sum(w, axis=0, keepdims=True)
                    weights[t].append(w.astype(jnp.bfloat16))
                m_ref[k, :, span] = top
                l_ref[k, :, span] = total
                shrinks.append(shrink)
            sums = [acc_ref[k, :, i * lanes : (i + 1) * lanes] * shrinks[i] for i in range(tiles)]
            for t in range(tiles):
                values = gathered[pl.ds(first, PLANE), pl.ds(at + units + 2 * t, 2)]
                values = values.reshape(keys_tile, head_size)
                w = jnp.concatenate(weights[t], 1)
                o = lax.dot_general(
                    values, w, (((0,), (0,)), ((), ())), preferred_element_type=jnp.float32
                )
                for i in range(t, tiles):
                    sums[i] += o[:, (i - t) * lanes : (i - t + 1) * lanes]
            for i in range(tiles):
                acc_ref[k, :, i * lanes : (i + 1) * lanes] = sums[i]

        for p in range(PIECES):
            for col in range(2):
                arrived(device(row, col, 1 - core), p)

            for i in range(per_piece):
                head(p * per_piece + i)

    def either(step, do):
        @pl.when(z >= step)
        def _():
            do(z - step, False)

        @pl.when(z + step < rows)
        def _():
            do(z + step, True)

    def relay_column(step):
        for p in range(PIECES):

            def do(row, from_above):
                slot = device(row, column, core)
                arrived(slot, p)
                if from_above:

                    @pl.when(z > 0)
                    def _():
                        copy(slot, p, below, 0).start()
                else:

                    @pl.when(z < rows - 1)
                    def _():
                        copy(slot, p, above, 3).start()
                share(slot, p)

            either(step, do)

    def relay_across(row):
        for p in range(PIECES):
            slot = device(row, 1 - column, core)
            arrived(slot, p)
            copy(slot, p, mate, 2).start()

    relay_column(1)
    relay_across(z)
    attend_plane(z)

    @pl.loop(1, rows)
    def _(step):
        @pl.when(step + 1 < rows)
        def _():
            relay_column(step + 1)

        either(step, lambda row, from_above: relay_across(row))
        either(step, lambda row, from_above: attend_plane(row))

    for k in range(kv_heads):
        o = (acc_ref[k] / l_ref[k]).T
        for t in range(tiles):
            for g in range(per_group):
                at = t * lanes + g * tile
                wide[pl.ds(t * tile * heads + k * per_group + g, tile, stride=heads), :] = o[at : at + tile]
    out_ref[...] = wide[...].astype(jnp.bfloat16)

    def sent(row, from_above):
        for p in range(PIECES):
            slot = device(row, column, core)
            if from_above:

                @pl.when(z > 0)
                def _():
                    copy(slot, p, below, 0).wait_send()
            else:

                @pl.when(z < rows - 1)
                def _():
                    copy(slot, p, above, 3).wait_send()
            copy(slot, p, across, 1).wait_send()
            copy(slot, p, mate, 2).wait_send()
            copy(device(row, 1 - column, core), p, mate, 2).wait_send()

    @pl.loop(1, rows)
    def _(step):
        either(step, sent)

    sent(z, False)
    for p in range(PIECES):

        @pl.when(z > 0)
        def _():
            copy(me, p, below, 0).wait_send()


def solution(mesh):
    n = mesh.shape["ctx"]

    def shards(queries, keys, values, positions):
        tokens, heads, head_size = queries.shape
        kv_heads = keys.shape[1]
        per_group = heads // kv_heads
        table = rotary_tables(tokens, head_size, n)
        tile = 2 * UNIT
        width = tokens * per_group
        blocks = 1 + 2 * (tokens // UNIT) * kv_heads
        vmem = pl.BlockSpec(memory_space=pltpu.VMEM)
        hbm = pl.BlockSpec(memory_space=pl.ANY)
        out = pl.pallas_call(
            functools.partial(attend, n, kv_heads, per_group, tokens),
            out_shape=jax.ShapeDtypeStruct((tokens * heads, head_size), jnp.bfloat16),
            in_specs=[hbm] * 5,
            out_specs=vmem,
            scratch_shapes=[
                pltpu.VMEM((n, blocks, UNIT, head_size), jnp.bfloat16),
                pltpu.VMEM((kv_heads, width, head_size), jnp.bfloat16),
                pltpu.VMEM((tokens * heads, head_size), jnp.float32),
                pltpu.VMEM((2, tokens * kv_heads, head_size), jnp.float32),
                pltpu.VMEM((kv_heads, 1, width), jnp.float32),
                pltpu.VMEM((kv_heads, 1, width), jnp.float32),
                pltpu.VMEM((kv_heads, head_size, width), jnp.float32),
                pltpu.SMEM((tokens,), jnp.int32),
                pltpu.VMEM((tokens * heads, head_size), jnp.bfloat16),
                pltpu.VMEM((tokens * kv_heads, head_size), jnp.bfloat16),
                pltpu.VMEM((tokens * kv_heads, head_size), jnp.bfloat16),
                pltpu.VMEM(table.shape, jnp.float32),
                pltpu.SemaphoreType.DMA((n, PIECES)),
                pltpu.SemaphoreType.DMA((4, n, PIECES)),
                pltpu.SemaphoreType.DMA((5,)),
            ],
            compiler_params=pltpu.CompilerParams(
                collective_id=0, has_side_effects=True, vmem_limit_bytes=48*1024*1024
            ),
        )(
            *(
                pltpu.with_memory_space_constraint(x, pltpu.HBM)
                for x in (
                    positions,
                    queries.reshape(tokens * heads, head_size),
                    keys.reshape(tokens * kv_heads, head_size),
                    values.reshape(tokens * kv_heads, head_size),
                    jnp.asarray(table),
                )
            )
        )
        return out.reshape(tokens, heads, head_size)

    placed = (
        P(("groups", "ctx"), None, None),
        P(("groups", "ctx"), None, None),
        P(("groups", "ctx"), None, None),
        P(("groups", "ctx")),
    )
    return jax.shard_map(
        shards,
        mesh=mesh,
        in_specs=placed,
        out_specs=P(("groups", "ctx"), None, None),
        check_vma=False,
    )
```

profile of v0, /device:TPU:0, one launch (start us, length us, event | category | flops | bytes accessed | tf_op | source)
XLA Modules:
  0.0 29.0 jit_solution(11272438724829362787)
XLA Ops:
  0.0 28.2 %shard_map.55 = bf16[1536,128]{1,0:T(8,128)(2,1)S(1)} custom-call(s32[96]{0:T(128)} %place_hbm.1, bf16[1536,128]{1,0:T(8,128)(2,1)} %bitcast.5, bf16[384,128]{1,0:T(8,128)(2,1)} %bitcast.6, bf16[384,128]{1,0:T(8,128)(2,1)} %bitcast.7, f32[200,128]{1,0:T(8,128)} %constant.2.clone.table_hbm), custom_call_target="tpu_custom_call" | custom-call | tf_op jit(solution)/shard_map/pallas_call | solution.py:314
  28.2 0.7 %copy.7 = bf16[96,16,128]{2,1,0:T(8,128)(2,1)} copy(bf16[96,16,128]{2,1,0:T(8,128)(2,1)S(1)} %bitcast.4) | data formatting | bytes 786432
where the time goes:
time: 29.1 us; the launch traced here: 29 us
  Pallas kernels  28.2 us (97%)
  local copies, waits for them, and re-layouts  0.75 us (3%)
    pallas_call x1, Pallas kernels, shards(): pl.pallas_call(functools.partial(attend, n, kv_heads, per_group, tokens),...  28.2 us
    unnamed x1, local copies, waits for them, and re-layouts  0.75 us

commit v1 on v0

v1 whole, which is shorter than its diff:
```python
import functools
import math

import jax
import jax.numpy as jnp
import numpy as np
from jax import lax
from jax.experimental import pallas as pl
from jax.experimental.pallas import tpu as pltpu
from jax.sharding import PartitionSpec as P

TILE = 32
DOWN, UP = 0, 1


def rotary_tables(tokens, head_size, stride):
    half = head_size // 2
    inverse = 1000000.0 ** (-2.0 * np.arange(half) / head_size)
    wide = lambda x: np.concatenate([x, x], -1)
    steps = (stride * np.arange(tokens))[:, None] * inverse[None, :]
    starts = np.arange(stride)[:, None] * inverse[None, :]
    return np.concatenate(
        [wide(np.cos(steps)), wide(np.sin(steps)), wide(np.cos(starts)), wide(np.sin(starts))]
    ).astype(np.float32)


def attend(
    n, kv_heads, per_group, tokens,
    place_hbm, q_hbm, k_hbm, v_hbm, table_hbm, out_ref,
    kv, kv_stage, q_all, q_stage, o_all, o_stage, offs, wide, small, m_ref, l_ref, acc_ref,
    place_ref, q_ref, k_ref, v_ref, table_ref,
    kv_recv, z_send, off_recv, offz_send, in_recv, in_send, inoff_recv, inoff_send,
    q_recv, q_send, o_recv, o_send, load_sem,
):
    loads = [
        pltpu.make_async_copy(src, dst, load_sem.at[i])
        for i, (src, dst) in enumerate(
            [(place_hbm, place_ref), (table_hbm, table_ref), (k_hbm, k_ref), (v_hbm, v_ref), (q_hbm, q_ref)]
        )
    ]
    for load in loads:
        load.start()
    head_size = q_ref.shape[-1]
    heads = kv_heads * per_group
    quartet = kv_heads
    rows = n // quartet
    pieces = tokens // TILE
    lanes = 2 * per_group * TILE
    factor = math.log2(math.e) / math.sqrt(head_size)
    me = lax.axis_index("ctx")
    z = me // quartet
    h = me % quartet
    column = h // 2
    core = h % 2
    mate = column * 2 + 1 - core
    across = (1 - column) * 2 + core
    diagonal = (1 - column) * 2 + 1 - core
    base = z * quartet
    targets = (me - quartet, me + quartet)
    onward = (z > 0, z < rows - 1)

    barrier = pltpu.get_barrier_semaphore()

    def greet(target):
        pl.semaphore_signal(barrier, inc=1, device_id={"ctx": target})

    for peer in (mate, across, diagonal):
        greet(base + peer)
    for way in (DOWN, UP):

        @pl.when(onward[way])
        def _():
            greet(targets[way])

    def remote(src, dst, send_sem, recv_sem, target):
        return pltpu.make_async_remote_copy(
            src_ref=src, dst_ref=dst, send_sem=send_sem, recv_sem=recv_sem, device_id={"ctx": target}
        )

    def piece(way, row, p, half, first=None, count=2):
        first = 2 * half if first is None else first
        part = kv.at[row, p, pl.ds(first, count)]
        return remote(part, part, z_send.at[way, row, p, half], kv_recv.at[row, p, half], targets[way])

    def mark(way, row, first=0, count=quartet):
        part = offs.at[row, pl.ds(first, count)]
        return remote(part, part, offz_send.at[way, row], off_recv.at[row], targets[way])

    def near(p, src, dst):
        return remote(kv_stage.at[dst, p], kv.at[z, p, src], in_send.at[p, dst], in_recv.at[p, src], base + dst)

    def near_mark(src, dst):
        part = offs.at[z, src]
        return remote(part, part, inoff_send.at[dst], inoff_recv.at[src], base + dst)

    def near_q(src, dst):
        return remote(
            q_stage.at[dst], q_all.at[src // 2, :, src % 2], q_send.at[dst], q_recv.at[src], base + dst
        )

    def back(p, src, dst):
        return remote(o_stage.at[p, dst], o_all.at[p, src], o_send.at[p, dst], o_recv.at[p, src], base + dst)

    for load in loads[:2]:
        load.wait()
    offset = place_ref[0]
    c0 = table_ref[pl.ds(2 * tokens + offset, 1), :]
    s0 = table_ref[pl.ds(2 * tokens + n + offset, 1), :]
    ct, st = table_ref[:tokens, :], table_ref[tokens : 2 * tokens, :]
    lane = lax.broadcasted_iota(jnp.int32, (tokens, head_size), 1)
    cosine = ct * c0 - st * s0
    sine = st * c0 + ct * s0
    sine = jnp.where(lane < head_size // 2, -sine, sine)

    def rotated(x):
        return (x * cosine + pltpu.roll(x, head_size // 2, 1) * sine).astype(jnp.bfloat16)

    offs[z, h] = jnp.full((1, head_size), offset.astype(jnp.float32), jnp.float32)
    for load in loads[2:4]:
        load.wait()
    small[0] = k_ref[...].astype(jnp.float32)
    small[1] = v_ref[...].astype(jnp.float32)
    for k in range(kv_heads):
        x = rotated(small[0, pl.ds(k, tokens, stride=kv_heads), :])
        kv_stage[k, :, 0] = x.reshape(pieces, TILE, head_size)
        x = small[1, pl.ds(k, tokens, stride=kv_heads), :].astype(jnp.bfloat16)
        kv_stage[k, :, 1] = x.reshape(pieces, TILE, head_size)
    for p in range(pieces):
        kv[z, p, h] = kv_stage[h, p]

    pl.semaphore_wait(barrier, 3 + onward[DOWN].astype(jnp.int32) + onward[UP].astype(jnp.int32))

    def spread(src):
        for way in (DOWN, UP):

            @pl.when(onward[way])
            def _():
                mark(way, z, src, 1).start()
                for p in range(pieces):
                    piece(way, z, p, src // 2, src, 1).start()

    for dst in (across, diagonal, mate):
        near_mark(h, dst).start()
    for p in range(pieces):
        for dst in (across, diagonal, mate):
            near(p, h, dst).start()
    spread(h)

    loads[4].wait()
    wide[...] = q_ref[...].astype(jnp.float32)
    for k in range(kv_heads):
        for g in range(per_group):
            q = rotated(wide[pl.ds(k * per_group + g, tokens, stride=heads), :])
            q_stage[k, :, g] = q.reshape(pieces, TILE, head_size)
    for dst in (across, diagonal, mate):
        near_q(h, dst).start()
    q_all[column, :, core] = q_stage[h]

    near_mark(mate, h).wait_recv()
    for p in range(pieces):
        near(p, mate, h).wait_recv()
    spread(mate)

    m_ref[...] = jnp.full(m_ref.shape, -jnp.inf, jnp.float32)
    l_ref[...] = jnp.zeros(l_ref.shape, jnp.float32)
    acc_ref[...] = jnp.zeros(acc_ref.shape, jnp.float32)

    for src in (across, diagonal):
        near_mark(src, h).wait_recv()
        for way in (DOWN, UP):

            @pl.when(onward[way])
            def _():
                mark(way, z, src, 1).start()

    for p in range(pieces):
        for src in (across, diagonal):
            near(p, src, h).wait_recv()
            for way in (DOWN, UP):

                @pl.when(onward[way])
                def _():
                    piece(way, z, p, src // 2, src, 1).start()

    keys_tile = quartet * TILE
    key_at = (lax.broadcasted_iota(jnp.int32, (keys_tile, lanes), 0) % TILE * n).astype(jnp.float32)
    query_at = (lax.broadcasted_iota(jnp.int32, (1, lanes), 1) % TILE * n).astype(jnp.float32)

    def attention(col, row, p):
        keys = kv[row, p, :, 0].reshape(keys_tile, head_size)
        values = kv[row, p, :, 1].reshape(keys_tile, head_size)
        first = p * lanes
        q = q_all[col, p:].reshape((pieces - p) * lanes, head_size)
        s = lax.dot_general(keys, q, (((1,), (1,)), ((), ())), preferred_element_type=jnp.float32)
        theirs = jnp.concatenate(
            [jnp.broadcast_to(jnp.concatenate([offs[row, i]] * (lanes // head_size), 1), (TILE, lanes)) for i in range(quartet)], 0
        )
        ours = jnp.concatenate(
            [jnp.concatenate([offs[z, 2 * col + i]] * (lanes // 2 // head_size), 1) for i in range(2)], 1
        )
        allowed = key_at + theirs <= query_at + ours
        head = jnp.where(allowed, s[:, :lanes], -jnp.inf)
        s = jnp.concatenate([head, s[:, lanes:]], 1) if p < pieces - 1 else head
        old = m_ref[col, :, first:]
        top = jnp.maximum(old, jnp.max(s, axis=0, keepdims=True))
        shrink = jnp.exp2((old - top) * factor)
        w = jnp.exp2((s - top) * factor)
        m_ref[col, :, first:] = top
        l_ref[col, :, first:] = l_ref[col, :, first:] * shrink + jnp.sum(w, axis=0, keepdims=True)
        o = lax.dot_general(
            values, w.astype(jnp.bfloat16), (((0,), (0,)), ((), ())), preferred_element_type=jnp.float32
        )
        acc_ref[col, :, first:] = acc_ref[col, :, first:] * shrink + o

    def events(k):
        return [(k - p, p) for p in reversed(range(pieces))]

    def each(k, do):
        for d, p in events(k):
            if isinstance(d, int) and not 1 <= d < rows:
                continue
            for way in (DOWN, UP):
                row = z + d if way == DOWN else z - d
                here = (row < rows) if way == DOWN else (row >= 0)
                if not isinstance(d, int):
                    here = here & (d >= 1) & (d < rows)

                @pl.when(here)
                def _():
                    do(way, row, p)

    def relay(k):
        def do(way, row, p):
            @pl.when(onward[way])
            def _():
                if p == 0:
                    mark(way, row).wait_recv()
                    mark(way, row).start()
                for half in (column, 1 - column):
                    piece(way, row, p, half).wait_recv()
                    piece(way, row, p, half).start()

        each(k, do)

    def take(k, cols, wait=True):
        def do(way, row, p):
            if wait:

                @pl.when(jnp.logical_not(onward[way]))
                def _():
                    if p == 0:
                        mark(way, row).wait_recv()
                    for half in (column, 1 - column):
                        piece(way, row, p, half).wait_recv()

            for col in cols:
                attention(col, row, p)

        each(k, do)

    def finish(p):
        for col in range(2):
            o = acc_ref[col, :, p * lanes : (p + 1) * lanes] / l_ref[col, :, p * lanes : (p + 1) * lanes]
            o = o.T.astype(jnp.bfloat16)
            for c in range(2):
                part = o[c * lanes // 2 : (c + 1) * lanes // 2]
                o_stage[p, 2 * col + c] = part.reshape(per_group, TILE, head_size)
        for dst in (across, diagonal, mate):
            back(p, h, dst).start()
        o_all[p, h] = o_stage[p, h]

    relay(1)
    for p in range(pieces):
        if p == 0:
            near_q(mate, h).wait_recv()
        attention(column, z, p)
    relay(2)
    take(1, [column])
    for src in (across, diagonal):
        near_q(src, h).wait_recv()
    for p in range(pieces):
        attention(1 - column, z, p)
    take(1, [1 - column], wait=False)

    @pl.loop(2, rows)
    def _(k):
        relay(k + 1)
        take(k, [0, 1])

    finish(0)
    for p in range(1, pieces):
        k = rows - 1 + p
        if p < pieces - 1:
            relay(k + 1)
        take(k, [0, 1])
        finish(p)

    for p in range(pieces):
        for src in (across, diagonal, mate):
            back(p, src, h).wait_recv()
        for k in range(kv_heads):
            for g in range(per_group):
                at = p * TILE * heads + k * per_group + g
                wide[pl.ds(at, TILE, stride=heads), :] = o_all[p, k, g].astype(jnp.float32)
        span = slice(p * TILE * heads, (p + 1) * TILE * heads)
        out_ref[span, :] = wide[span, :].astype(jnp.bfloat16)

    for dst in (across, diagonal, mate):
        near_mark(h, dst).wait_send()
        near_q(h, dst).wait_send()
        for p in range(pieces):
            near(p, h, dst).wait_send()
            back(p, h, dst).wait_send()

    def sent(way, row):
        @pl.when(onward[way])
        def _():
            mark(way, row).wait_send()
            for p in range(pieces):
                for half in range(2):
                    piece(way, row, p, half).wait_send()

    for way in (DOWN, UP):
        sent(way, z)

    @pl.loop(1, rows)
    def _(d):
        @pl.when(z + d < rows)
        def _():
            sent(DOWN, z + d)

        @pl.when(z - d >= 0)
        def _():
            sent(UP, z - d)


def solution(mesh):
    n = mesh.shape["ctx"]

    def shards(queries, keys, values, positions):
        tokens, heads, head_size = queries.shape
        kv_heads = keys.shape[1]
        per_group = heads // kv_heads
        table = rotary_tables(tokens, head_size, n)
        pieces = tokens // TILE
        rows = n // kv_heads
        width = 2 * per_group * tokens
        vmem = pl.BlockSpec(memory_space=pltpu.VMEM)
        hbm = pl.BlockSpec(memory_space=pl.ANY)
        dma = pltpu.SemaphoreType.DMA
        bf16, f32 = jnp.bfloat16, jnp.float32
        out = pl.pallas_call(
            functools.partial(attend, n, kv_heads, per_group, tokens),
            out_shape=jax.ShapeDtypeStruct((tokens * heads, head_size), bf16),
            in_specs=[hbm] * 5,
            out_specs=vmem,
            scratch_shapes=[
                pltpu.VMEM((rows, pieces, kv_heads, 2, TILE, head_size), bf16),
                pltpu.VMEM((kv_heads, pieces, 2, TILE, head_size), bf16),
                pltpu.VMEM((2, pieces, 2, per_group, TILE, head_size), bf16),
                pltpu.VMEM((kv_heads, pieces, per_group, TILE, head_size), bf16),
                pltpu.VMEM((pieces, kv_heads, per_group, TILE, head_size), bf16),
                pltpu.VMEM((pieces, kv_heads, per_group, TILE, head_size), bf16),
                pltpu.VMEM((rows, kv_heads, 1, head_size), f32),
                pltpu.VMEM((tokens * heads, head_size), f32),
                pltpu.VMEM((2, tokens * kv_heads, head_size), f32),
                pltpu.VMEM((2, 1, width), f32),
                pltpu.VMEM((2, 1, width), f32),
                pltpu.VMEM((2, head_size, width), f32),
                pltpu.SMEM((tokens,), jnp.int32),
                pltpu.VMEM((tokens * heads, head_size), bf16),
                pltpu.VMEM((tokens * kv_heads, head_size), bf16),
                pltpu.VMEM((tokens * kv_heads, head_size), bf16),
                pltpu.VMEM(table.shape, f32),
                dma((rows, pieces, 2)),
                dma((2, rows, pieces, 2)),
                dma((rows,)),
                dma((2, rows)),
                dma((pieces, kv_heads)),
                dma((pieces, kv_heads)),
                dma((kv_heads,)),
                dma((kv_heads,)),
                dma((kv_heads,)),
                dma((kv_heads,)),
                dma((pieces, kv_heads)),
                dma((pieces, kv_heads)),
                dma((5,)),
            ],
            compiler_params=pltpu.CompilerParams(
                collective_id=0, has_side_effects=True, vmem_limit_bytes=48 * 1024 * 1024
            ),
        )(
            *(
                pltpu.with_memory_space_constraint(x, pltpu.HBM)
                for x in (
                    positions,
                    queries.reshape(tokens * heads, head_size),
                    keys.reshape(tokens * kv_heads, head_size),
                    values.reshape(tokens * kv_heads, head_size),
                    jnp.asarray(table),
                )
            )
        )
        return out.reshape(tokens, heads, head_size)

    placed = (
        P(("groups", "ctx"), None, None),
        P(("groups", "ctx"), None, None),
        P(("groups", "ctx"), None, None),
        P(("groups", "ctx")),
    )
    return jax.shard_map(
        shards,
        mesh=mesh,
        in_specs=placed,
        out_specs=P(("groups", "ctx"), None, None),
        check_vma=False,
    )
```

time: 29.1 us -> 29.3 us (level)
  no operation moved by 1% of the time
where the time goes in v1:
time: 29.3 us; the launch traced here: 29.2 us
  Pallas kernels  28.4 us (97%)
  local copies, waits for them, and re-layouts  0.75 us (3%)
    pallas_call x1, Pallas kernels, shards(): pl.pallas_call(functools.partial(attend, n, kv_heads, per_group, tokens),...  28.4 us
    unnamed x1, local copies, waits for them, and re-layouts  0.75 us

profile of v1, /device:TPU:0, one launch (start us, length us, event | category | flops | bytes accessed | tf_op | source)
XLA Modules:
  0.0 29.2 jit_solution(11100421560758511997)
XLA Ops:
  0.0 28.4 %shard_map.55 = bf16[1536,128]{1,0:T(8,128)(2,1)S(1)} custom-call(s32[96]{0:T(128)} %place_hbm.1, bf16[1536,128]{1,0:T(8,128)(2,1)} %bitcast.5, bf16[384,128]{1,0:T(8,128)(2,1)} %bitcast.6, bf16[384,128]{1,0:T(8,128)(2,1)} %bitcast.7, f32[224,128]{1,0:T(8,128)} %constant.2.clone.table_hbm), custom_call_target="tpu_custom_call" | custom-call | tf_op jit(solution)/shard_map/pallas_call | solution.py:352
  28.4 0.7 %copy.7 = bf16[96,16,128]{2,1,0:T(8,128)(2,1)} copy(bf16[96,16,128]{2,1,0:T(8,128)(2,1)S(1)} %bitcast.4) | data formatting | bytes 786432

commit v2 on v1

--- a/solution.py
+++ b/solution.py
@@ -11,6 +11,7 @@
 
 TILE = 32
 DOWN, UP = 0, 1
+FAR = 3
 
 
 def rotary_tables(tokens, head_size, stride):
@@ -29,7 +30,7 @@
     place_hbm, q_hbm, k_hbm, v_hbm, table_hbm, out_ref,
     kv, kv_stage, q_all, q_stage, o_all, o_stage, offs, wide, small, m_ref, l_ref, acc_ref,
     place_ref, q_ref, k_ref, v_ref, table_ref,
-    kv_recv, z_send, off_recv, offz_send, in_recv, in_send, inoff_recv, inoff_send,
+    kv_recv, z_send, far_send, off_recv, offz_send, offfar_send, in_recv, in_send, inoff_recv, inoff_send,
     q_recv, q_send, o_recv, o_send, load_sem,
 ):
     loads = [
@@ -56,21 +57,28 @@
     across = (1 - column) * 2 + core
     diagonal = (1 - column) * 2 + 1 - core
     base = z * quartet
-    targets = (me - quartet, me + quartet)
-    onward = (z > 0, z < rows - 1)
+
+    def target(way, step):
+        return me - step * quartet if way == DOWN else me + step * quartet
+
+    def reaches(way, step):
+        return z >= step if way == DOWN else z + step < rows
 
     barrier = pltpu.get_barrier_semaphore()
 
-    def greet(target):
-        pl.semaphore_signal(barrier, inc=1, device_id={"ctx": target})
+    def greet(peer):
+        pl.semaphore_signal(barrier, inc=1, device_id={"ctx": peer})
 
     for peer in (mate, across, diagonal):
         greet(base + peer)
+    greeted = 3
     for way in (DOWN, UP):
-
-        @pl.when(onward[way])
-        def _():
-            greet(targets[way])
+        for step in (1, FAR):
+            greeted += reaches(way, step).astype(jnp.int32)
+
+            @pl.when(reaches(way, step))
+            def _():
+                greet(target(way, step))
 
     def remote(src, dst, send_sem, recv_sem, target):
         return pltpu.make_async_remote_copy(
@@ -80,11 +88,20 @@
     def piece(way, row, p, half, first=None, count=2):
         first = 2 * half if first is None else first
         part = kv.at[row, p, pl.ds(first, count)]
-        return remote(part, part, z_send.at[way, row, p, half], kv_recv.at[row, p, half], targets[way])
+        return remote(part, part, z_send.at[way, row, p, half], kv_recv.at[row, p, half], target(way, 1))
 
     def mark(way, row, first=0, count=quartet):
         part = offs.at[row, pl.ds(first, count)]
-        return remote(part, part, offz_send.at[way, row], off_recv.at[row], targets[way])
+        return remote(part, part, offz_send.at[way, row], off_recv.at[row], target(way, 1))
+
+    def far_piece(way, p, half, first=None, count=2):
+        first = 2 * half if first is None else first
+        part = kv.at[z, p, pl.ds(first, count)]
+        return remote(part, part, far_send.at[way, p, half], kv_recv.at[z, p, half], target(way, FAR))
+
+    def far_mark(way, first=0, count=quartet):
+        part = offs.at[z, pl.ds(first, count)]
+        return remote(part, part, offfar_send.at[way], off_recv.at[z], target(way, FAR))
 
     def near(p, src, dst):
         return remote(kv_stage.at[dst, p], kv.at[z, p, src], in_send.at[p, dst], in_recv.at[p, src], base + dst)
@@ -95,7 +112,7 @@
 
     def near_q(src, dst):
         return remote(
-            q_stage.at[dst], q_all.at[src // 2, :, src % 2], q_send.at[dst], q_recv.at[src], base + dst
+            q_stage.at[dst], q_all.at[:, src // 2, src % 2], q_send.at[dst], q_recv.at[src], base + dst
         )
 
     def back(p, src, dst):
@@ -128,15 +145,23 @@
     for p in range(pieces):
         kv[z, p, h] = kv_stage[h, p]
 
-    pl.semaphore_wait(barrier, 3 + onward[DOWN].astype(jnp.int32) + onward[UP].astype(jnp.int32))
-
-    def spread(src):
+    pl.semaphore_wait(barrier, greeted)
+
+    def spread(src, which, marks):
         for way in (DOWN, UP):
 
-            @pl.when(onward[way])
-            def _():
-                mark(way, z, src, 1).start()
-                for p in range(pieces):
+            @pl.when(reaches(way, FAR))
+            def _():
+                if marks:
+                    far_mark(way, src, 1).start()
+                for p in which:
+                    far_piece(way, p, src // 2, src, 1).start()
+
+            @pl.when(reaches(way, 1))
+            def _():
+                if marks:
+                    mark(way, z, src, 1).start()
+                for p in which:
                     piece(way, z, p, src // 2, src, 1).start()
 
     for dst in (across, diagonal, mate):
@@ -144,7 +169,7 @@
     for p in range(pieces):
         for dst in (across, diagonal, mate):
             near(p, h, dst).start()
-    spread(h)
+    spread(h, range(pieces), True)
 
     loads[4].wait()
     wide[...] = q_ref[...].astype(jnp.float32)
@@ -154,84 +179,84 @@
             q_stage[k, :, g] = q.reshape(pieces, TILE, head_size)
     for dst in (across, diagonal, mate):
         near_q(h, dst).start()
-    q_all[column, :, core] = q_stage[h]
+    q_all[:, column, core] = q_stage[h]
 
     near_mark(mate, h).wait_recv()
     for p in range(pieces):
         near(p, mate, h).wait_recv()
-    spread(mate)
+    spread(mate, range(pieces), True)
 
     m_ref[...] = jnp.full(m_ref.shape, -jnp.inf, jnp.float32)
     l_ref[...] = jnp.zeros(l_ref.shape, jnp.float32)
     acc_ref[...] = jnp.zeros(acc_ref.shape, jnp.float32)
 
-    for src in (across, diagonal):
-        near_mark(src, h).wait_recv()
-        for way in (DOWN, UP):
-
-            @pl.when(onward[way])
-            def _():
-                mark(way, z, src, 1).start()
-
     for p in range(pieces):
         for src in (across, diagonal):
+            if p == 0:
+                near_mark(src, h).wait_recv()
             near(p, src, h).wait_recv()
-            for way in (DOWN, UP):
-
-                @pl.when(onward[way])
-                def _():
-                    piece(way, z, p, src // 2, src, 1).start()
+            spread(src, [p], p == 0)
 
     keys_tile = quartet * TILE
     key_at = (lax.broadcasted_iota(jnp.int32, (keys_tile, lanes), 0) % TILE * n).astype(jnp.float32)
     query_at = (lax.broadcasted_iota(jnp.int32, (1, lanes), 1) % TILE * n).astype(jnp.float32)
 
-    def attention(col, row, p):
+    def attention(cols, row, p):
         keys = kv[row, p, :, 0].reshape(keys_tile, head_size)
         values = kv[row, p, :, 1].reshape(keys_tile, head_size)
-        first = p * lanes
-        q = q_all[col, p:].reshape((pieces - p) * lanes, head_size)
-        s = lax.dot_general(keys, q, (((1,), (1,)), ((), ())), preferred_element_type=jnp.float32)
+        blocks = [(i, col) for i in range(p, pieces) for col in cols]
+        q = jnp.concatenate([q_all[i, col].reshape(lanes, head_size) for i, col in blocks], 0)
+        scores = lax.dot_general(keys, q, (((1,), (1,)), ((), ())), preferred_element_type=jnp.float32)
         theirs = jnp.concatenate(
-            [jnp.broadcast_to(jnp.concatenate([offs[row, i]] * (lanes // head_size), 1), (TILE, lanes)) for i in range(quartet)], 0
-        )
-        ours = jnp.concatenate(
-            [jnp.concatenate([offs[z, 2 * col + i]] * (lanes // 2 // head_size), 1) for i in range(2)], 1
-        )
-        allowed = key_at + theirs <= query_at + ours
-        head = jnp.where(allowed, s[:, :lanes], -jnp.inf)
-        s = jnp.concatenate([head, s[:, lanes:]], 1) if p < pieces - 1 else head
-        old = m_ref[col, :, first:]
-        top = jnp.maximum(old, jnp.max(s, axis=0, keepdims=True))
-        shrink = jnp.exp2((old - top) * factor)
-        w = jnp.exp2((s - top) * factor)
-        m_ref[col, :, first:] = top
-        l_ref[col, :, first:] = l_ref[col, :, first:] * shrink + jnp.sum(w, axis=0, keepdims=True)
+            [
+                jnp.broadcast_to(jnp.concatenate([offs[row, i]] * (lanes // head_size), 1), (TILE, lanes))
+                for i in range(quartet)
+            ],
+            0,
+        )
+        key_place = key_at + theirs
+        weights, shrinks = [], []
+        for at, (i, col) in enumerate(blocks):
+            s = scores[:, at * lanes : (at + 1) * lanes]
+            if i == p:
+                ours = jnp.concatenate(
+                    [jnp.concatenate([offs[z, 2 * col + c]] * (lanes // 2 // head_size), 1) for c in range(2)], 1
+                )
+                s = jnp.where(key_place <= query_at + ours, s, -jnp.inf)
+            old = m_ref[i, col]
+            top = jnp.maximum(old, jnp.max(s, axis=0, keepdims=True))
+            shrink = jnp.exp2((old - top) * factor)
+            w = jnp.exp2((s - top) * factor)
+            m_ref[i, col] = top
+            l_ref[i, col] = l_ref[i, col] * shrink + jnp.sum(w, axis=0, keepdims=True)
+            weights.append(w.astype(jnp.bfloat16))
+            shrinks.append(shrink)
         o = lax.dot_general(
-            values, w.astype(jnp.bfloat16), (((0,), (0,)), ((), ())), preferred_element_type=jnp.float32
-        )
-        acc_ref[col, :, first:] = acc_ref[col, :, first:] * shrink + o
-
-    def events(k):
-        return [(k - p, p) for p in reversed(range(pieces))]
-
-    def each(k, do):
-        for d, p in events(k):
-            if isinstance(d, int) and not 1 <= d < rows:
-                continue
-            for way in (DOWN, UP):
-                row = z + d if way == DOWN else z - d
-                here = (row < rows) if way == DOWN else (row >= 0)
-                if not isinstance(d, int):
-                    here = here & (d >= 1) & (d < rows)
-
-                @pl.when(here)
-                def _():
-                    do(way, row, p)
-
-    def relay(k):
-        def do(way, row, p):
-            @pl.when(onward[way])
+            values, jnp.concatenate(weights, 1), (((0,), (0,)), ((), ())), preferred_element_type=jnp.float32
+        )
+        for at, (i, col) in enumerate(blocks):
+            acc_ref[i, col] = acc_ref[i, col] * shrinks[at] + o[:, at * lanes : (at + 1) * lanes]
+
+    def relayed(way, d):
+        return reaches(way, 1) & ((d == 1) | (d >= FAR))
+
+    def arrive(way, row, p):
+        if p == 0:
+            mark(way, row).wait_recv()
+        for half in (column, 1 - column):
+            piece(way, row, p, half).wait_recv()
+
+    def each(d, do):
+        for way in (DOWN, UP):
+            row = z + d if way == DOWN else z - d
+
+            @pl.when((row < rows) if way == DOWN else (row >= 0))
+            def _():
+                do(way, row)
+
+    def relay(d, p):
+        def do(way, row):
+            @pl.when(relayed(way, d))
             def _():
                 if p == 0:
                     mark(way, row).wait_recv()
@@ -240,27 +265,21 @@
                     piece(way, row, p, half).wait_recv()
                     piece(way, row, p, half).start()
 
-        each(k, do)
-
-    def take(k, cols, wait=True):
-        def do(way, row, p):
-            if wait:
-
-                @pl.when(jnp.logical_not(onward[way]))
-                def _():
-                    if p == 0:
-                        mark(way, row).wait_recv()
-                    for half in (column, 1 - column):
-                        piece(way, row, p, half).wait_recv()
-
-            for col in cols:
-                attention(col, row, p)
-
-        each(k, do)
+        each(d, do)
+
+    def take(d, p):
+        def do(way, row):
+            @pl.when(jnp.logical_not(relayed(way, d)))
+            def _():
+                arrive(way, row, p)
+
+            attention((0, 1), row, p)
+
+        each(d, do)
 
     def finish(p):
         for col in range(2):
-            o = acc_ref[col, :, p * lanes : (p + 1) * lanes] / l_ref[col, :, p * lanes : (p + 1) * lanes]
+            o = acc_ref[p, col] * (1.0 / l_ref[p, col])
             o = o.T.astype(jnp.bfloat16)
             for c in range(2):
                 part = o[c * lanes // 2 : (c + 1) * lanes // 2]
@@ -269,30 +288,32 @@
             back(p, h, dst).start()
         o_all[p, h] = o_stage[p, h]
 
-    relay(1)
-    for p in range(pieces):
-        if p == 0:
-            near_q(mate, h).wait_recv()
-        attention(column, z, p)
-    relay(2)
-    take(1, [column])
+    near_q(mate, h).wait_recv()
+    for p in range(pieces):
+        attention([column], z, p)
+    relay(1, 0)
+    relay(1, 1)
     for src in (across, diagonal):
         near_q(src, h).wait_recv()
     for p in range(pieces):
-        attention(1 - column, z, p)
-    take(1, [1 - column], wait=False)
-
-    @pl.loop(2, rows)
-    def _(k):
-        relay(k + 1)
-        take(k, [0, 1])
-
-    finish(0)
-    for p in range(1, pieces):
-        k = rows - 1 + p
-        if p < pieces - 1:
-            relay(k + 1)
-        take(k, [0, 1])
+        attention([1 - column], z, p)
+        if p == 0:
+            for last in range(2, pieces):
+                relay(1, last)
+
+    if rows > FAR + 1:
+        for p in range(pieces):
+            relay(FAR, p)
+
+        @pl.loop(FAR + 1, rows)
+        def _(d):
+            for p in range(pieces):
+                relay(d, p)
+                take(d, p)
+
+    for p in range(pieces):
+        for d in (1, 3, 2):
+            take(d, p)
         finish(p)
 
     for p in range(pieces):
@@ -312,8 +333,8 @@
             near(p, h, dst).wait_send()
             back(p, h, dst).wait_send()
 
-    def sent(way, row):
-        @pl.when(onward[way])
+    def sent(way, row, d):
+        @pl.when(reaches(way, 1) if d is None else relayed(way, d))
         def _():
             mark(way, row).wait_send()
             for p in range(pieces):
@@ -321,17 +342,24 @@
                     piece(way, row, p, half).wait_send()
 
     for way in (DOWN, UP):
-        sent(way, z)
+        sent(way, z, None)
+
+        @pl.when(reaches(way, FAR))
+        def _():
+            far_mark(way).wait_send()
+            for p in range(pieces):
+                for half in range(2):
+                    far_piece(way, p, half).wait_send()
 
     @pl.loop(1, rows)
     def _(d):
         @pl.when(z + d < rows)
         def _():
-            sent(DOWN, z + d)
+            sent(DOWN, z + d, d)
 
         @pl.when(z - d >= 0)
         def _():
-            sent(UP, z - d)
+            sent(UP, z - d, d)
 
 
 def solution(mesh):
@@ -344,7 +372,7 @@
         table = rotary_tables(tokens, head_size, n)
         pieces = tokens // TILE
         rows = n // kv_heads
-        width = 2 * per_group * tokens
+        lanes = 2 * per_group * TILE
         vmem = pl.BlockSpec(memory_space=pltpu.VMEM)
         hbm = pl.BlockSpec(memory_space=pl.ANY)
         dma = pltpu.SemaphoreType.DMA
@@ -357,16 +385,16 @@
             scratch_shapes=[
                 pltpu.VMEM((rows, pieces, kv_heads, 2, TILE, head_size), bf16),
                 pltpu.VMEM((kv_heads, pieces, 2, TILE, head_size), bf16),
-                pltpu.VMEM((2, pieces, 2, per_group, TILE, head_size), bf16),
+                pltpu.VMEM((pieces, 2, 2, per_group, TILE, head_size), bf16),
                 pltpu.VMEM((kv_heads, pieces, per_group, TILE, head_size), bf16),
                 pltpu.VMEM((pieces, kv_heads, per_group, TILE, head_size), bf16),
                 pltpu.VMEM((pieces, kv_heads, per_group, TILE, head_size), bf16),
                 pltpu.VMEM((rows, kv_heads, 1, head_size), f32),
                 pltpu.VMEM((tokens * heads, head_size), f32),
                 pltpu.VMEM((2, tokens * kv_heads, head_size), f32),
-                pltpu.VMEM((2, 1, width), f32),
-                pltpu.VMEM((2, 1, width), f32),
-                pltpu.VMEM((2, head_size, width), f32),
+                pltpu.VMEM((pieces, 2, 1, lanes), f32),
+                pltpu.VMEM((pieces, 2, 1, lanes), f32),
+                pltpu.VMEM((pieces, 2, head_size, lanes), f32),
                 pltpu.SMEM((tokens,), jnp.int32),
                 pltpu.VMEM((tokens * heads, head_size), bf16),
                 pltpu.VMEM((tokens * kv_heads, head_size), bf16),
@@ -374,8 +402,10 @@
                 pltpu.VMEM(table.shape, f32),
                 dma((rows, pieces, 2)),
                 dma((2, rows, pieces, 2)),
+                dma((2, pieces, 2)),
                 dma((rows,)),
                 dma((2, rows)),
+                dma((2,)),
                 dma((pieces, kv_heads)),
                 dma((pieces, kv_heads)),
                 dma((kv_heads,)),

time: 29.3 us -> 25.9 us (0.88)
  Pallas kernels: 28.4 us -> 25 us
    pallas_call x1, Pallas kernels: 28.4 us -> 25 us  [shards(): pl.pallas_call(functools.partial(attend, n, kv_heads, per_group, tokens),...]
where the time goes in v2:
time: 25.9 us; the launch traced here: 25.7 us
  Pallas kernels  25 us (97%)
  local copies, waits for them, and re-layouts  0.75 us (3%)
    pallas_call x1, Pallas kernels, shards(): pl.pallas_call(functools.partial(attend, n, kv_heads, per_group, tokens),...  25 us
    unnamed x1, local copies, waits for them, and re-layouts  0.75 us

profile of v2, /device:TPU:0, one launch (start us, length us, event | category | flops | bytes accessed | tf_op | source)
XLA Modules:
  0.0 25.7 jit_solution(10793586434793858711)
XLA Ops:
  0.0 25.0 %shard_map.55 = bf16[1536,128]{1,0:T(8,128)(2,1)S(1)} custom-call(s32[96]{0:T(128)} %place_hbm.1, bf16[1536,128]{1,0:T(8,128)(2,1)} %bitcast.5, bf16[384,128]{1,0:T(8,128)(2,1)} %bitcast.6, bf16[384,128]{1,0:T(8,128)(2,1)} %bitcast.7, f32[224,128]{1,0:T(8,128)} %constant.2.clone.table_hbm), custom_call_target="tpu_custom_call" | custom-call | tf_op jit(solution)/shard_map/pallas_call | solution.py:380
  25.0 0.7 %copy.7 = bf16[96,16,128]{2,1,0:T(8,128)(2,1)} copy(bf16[96,16,128]{2,1,0:T(8,128)(2,1)S(1)} %bitcast.4) | data formatting | bytes 786432

commit v3 on v2

v3 whole, which is shorter than its diff:
```python
import functools
import math

import jax
import jax.numpy as jnp
import numpy as np
from jax import lax
from jax.experimental import pallas as pl
from jax.experimental.pallas import tpu as pltpu
from jax.sharding import PartitionSpec as P

UNIT = 16
DOWN, UP = 0, 1
FAR = 3


def rotary_tables(tokens, head_size, stride):
    half = head_size // 2
    inverse = 1000000.0 ** (-2.0 * np.arange(half) / head_size)
    wide = lambda x: np.concatenate([x, x], -1)
    steps = (stride * np.arange(tokens))[:, None] * inverse[None, :]
    starts = np.arange(stride)[:, None] * inverse[None, :]
    return np.concatenate(
        [wide(np.cos(steps)), wide(np.sin(steps)), wide(np.cos(starts)), wide(np.sin(starts))]
    ).astype(np.float32)


def cuts(units):
    whole = [(u, min(u + 2, units)) for u in range(0, units, 2)]
    last = whole[-1]
    return whole, whole[:-1] + [(u, u + 1) for u in range(*last)]


def attend(
    n, kv_heads, per_group, tokens,
    place_hbm, q_hbm, k_hbm, v_hbm, table_hbm, out_ref,
    kv, kv_stage, q_all, q_stage, o_all, o_stage, offs, wide, small, m_ref, l_ref, acc_ref,
    place_ref, q_ref, k_ref, v_ref, table_ref,
    kv_recv, z_send, far_send, off_recv, offz_send, in_recv, in_send, inoff_recv, inoff_send,
    q_recv, q_send, o_recv, o_send, alive, load_sem,
):
    loads = [
        pltpu.make_async_copy(src, dst, load_sem.at[i])
        for i, (src, dst) in enumerate(
            [(place_hbm, place_ref), (table_hbm, table_ref), (k_hbm, k_ref), (v_hbm, v_ref), (q_hbm, q_ref)]
        )
    ]
    for load in loads:
        load.start()
    head_size = q_ref.shape[-1]
    heads = kv_heads * per_group
    quartet = kv_heads
    rows = n // quartet
    units = tokens // UNIT
    steps, pieces = cuts(units)
    lanes = 2 * per_group * UNIT
    factor = math.log2(math.e) / math.sqrt(head_size)
    me = lax.axis_index("ctx")
    z = me // quartet
    h = me % quartet
    column = h // 2
    core = h % 2
    mate = column * 2 + 1 - core
    across = (1 - column) * 2 + core
    diagonal = (1 - column) * 2 + 1 - core
    base = z * quartet

    def target(way, step):
        return me - step * quartet if way == DOWN else me + step * quartet

    def reaches(way, step):
        return z >= step if way == DOWN else z + step < rows

    barrier = pltpu.get_barrier_semaphore()

    def greet(peer):
        pl.semaphore_signal(barrier, inc=1, device_id={"ctx": peer})

    for peer in (mate, across, diagonal):
        greet(base + peer)
    greeted = 3 + reaches(DOWN, FAR).astype(jnp.int32)
    for way in (DOWN, UP):
        greeted += reaches(way, 1).astype(jnp.int32)

        @pl.when(reaches(way, 1))
        def _():
            greet(target(way, 1))

    @pl.when(reaches(UP, FAR))
    def _():
        greet(target(UP, FAR))

    def remote(src, dst, send_sem, recv_sem, target):
        return pltpu.make_async_remote_copy(
            src_ref=src, dst_ref=dst, send_sem=send_sem, recv_sem=recv_sem, device_id={"ctx": target}
        )

    def part_of(row, i, first, count):
        u0, u1 = pieces[i]
        return kv.at[row, pl.ds(u0, u1 - u0), pl.ds(first, count)]

    def slot(row):
        d = jnp.abs(row - z)
        return jnp.where(d > 1, d - 1, d)

    def piece(way, row, i, half, first=None, count=2):
        part = part_of(row, i, 2 * half if first is None else first, count)
        return remote(part, part, z_send.at[way, slot(row)], kv_recv.at[row, i, half], target(way, 1))

    def far_piece(way, i, half, first=None, count=2):
        part = part_of(z, i, 2 * half if first is None else first, count)
        return remote(part, part, far_send.at[way], kv_recv.at[z, i, half], target(way, FAR))

    def mark(way, row, first=0, count=quartet):
        part = offs.at[row, pl.ds(first, count)]
        return remote(part, part, offz_send.at[way, slot(row)], off_recv.at[row], target(way, 1))

    def far_mark(way, first=0, count=quartet):
        part = offs.at[z, pl.ds(first, count)]
        return remote(part, part, far_send.at[2 + way], off_recv.at[z], target(way, FAR))

    def near(i, src, dst):
        u0, u1 = pieces[i]
        span = pl.ds(u0, u1 - u0)
        return remote(kv_stage.at[dst, span], kv.at[z, span, src], in_send, in_recv.at[i], base + dst)

    def near_whole(src, dst):
        return remote(kv_stage.at[dst], kv.at[z, :, src], in_send, in_recv.at[len(pieces)], base + dst)

    def near_mark(src, dst, mine):
        part = offs.at[z, src]
        return remote(part, part, inoff_send, inoff_recv.at[mine], base + dst)

    def near_q(src, dst, mine):
        return remote(q_stage.at[dst], q_all.at[:, src // 2, src % 2], q_send, q_recv.at[mine], base + dst)

    def back(i, src, dst):
        u0, u1 = pieces[i]
        span = pl.ds(u0, u1 - u0)
        return remote(o_stage.at[span, dst], o_all.at[span, src], o_send, o_recv.at[i], base + dst)

    def waits(ref, send=None, recv=None):
        copy = remote(ref, ref, in_send if send is None else send, in_send if recv is None else recv, me)
        copy.wait_send() if recv is None else copy.wait_recv()

    for load in loads[:2]:
        load.wait()
    offset = place_ref[0]
    c0 = table_ref[pl.ds(2 * tokens + offset, 1), :]
    s0 = table_ref[pl.ds(2 * tokens + n + offset, 1), :]
    ct, st = table_ref[:tokens, :], table_ref[tokens : 2 * tokens, :]
    lane = lax.broadcasted_iota(jnp.int32, (tokens, head_size), 1)
    cosine = ct * c0 - st * s0
    sine = st * c0 + ct * s0
    sine = jnp.where(lane < head_size // 2, -sine, sine)

    def rotated(x):
        return (x * cosine + pltpu.roll(x, head_size // 2, 1) * sine).astype(jnp.bfloat16)

    offs[z, h] = jnp.full((1, head_size), offset.astype(jnp.float32), jnp.float32)
    for load in loads[2:4]:
        load.wait()
    small[0] = k_ref[...].astype(jnp.float32)
    small[1] = v_ref[...].astype(jnp.float32)
    for k in range(kv_heads):
        x = rotated(small[0, pl.ds(k, tokens, stride=kv_heads), :])
        kv_stage[k, :, 0] = x.reshape(units, UNIT, head_size)
        x = small[1, pl.ds(k, tokens, stride=kv_heads), :].astype(jnp.bfloat16)
        kv_stage[k, :, 1] = x.reshape(units, UNIT, head_size)
    kv[z, :, h] = kv_stage[h]

    pl.semaphore_wait(barrier, greeted)

    @pl.when(reaches(DOWN, FAR))
    def _():
        pl.semaphore_signal(alive, inc=1, device_id={"ctx": target(DOWN, FAR)})

    def spread(which, half, first, count, marks):
        @pl.when(reaches(DOWN, FAR))
        def _():
            if marks:
                far_mark(DOWN, first, count).start()
            for i in which:
                far_piece(DOWN, i, half, first, count).start()

        for way in (DOWN, UP):

            @pl.when(reaches(way, 1))
            def _():
                if marks:
                    mark(way, z, first, count).start()
                for i in which:
                    piece(way, z, i, half, first, count).start()

    every = range(len(pieces))
    for dst in (across, diagonal):
        near_mark(h, dst, 0).start()
    for i in every:
        for dst in (across, diagonal):
            near(i, h, dst).start()
    near_mark(h, mate, 1).start()
    near_whole(h, mate).start()
    spread(every, column, h, 1, True)

    loads[4].wait()
    wide[...] = q_ref[...].astype(jnp.float32)
    for k in range(kv_heads):
        for g in range(per_group):
            q = rotated(wide[pl.ds(k * per_group + g, tokens, stride=heads), :])
            q_stage[k, :, g] = q.reshape(units, UNIT, head_size)
    for dst in (across, diagonal):
        near_q(h, dst, 0).start()
    near_q(h, mate, 1).start()
    q_all[:, column, core] = q_stage[h]

    near_mark(mate, h, 1).wait_recv()
    near_whole(mate, h).wait_recv()
    spread(every, column, mate, 1, True)

    other = 1 - column
    for i in every:
        if i == 0:
            waits(offs.at[z, pl.ds(2 * other, 2)], recv=inoff_recv.at[0])
        waits(part_of(z, i, 2 * other, 2), recv=in_recv.at[i])
        spread([i], other, 2 * other, 2, i == 0)

    @pl.when(reaches(UP, FAR))
    def _():
        pl.semaphore_wait(alive, 1)
        far_mark(UP).start()
        for i in every:
            for half in (column, other):
                far_piece(UP, i, half).start()

    query_at = (lax.broadcasted_iota(jnp.int32, (1, lanes), 1) % UNIT * n).astype(jnp.float32)
    first_core = lax.broadcasted_iota(jnp.int32, (1, lanes), 1) < lanes // 2

    def attention(cols, row, step, fresh=False):
        u0, u1 = step
        below, count = u0 * quartet * UNIT, u1 * quartet * UNIT
        keys = kv[row, :u1, :, 0].reshape(count, head_size)
        values = kv[row, :u1, :, 1].reshape(count, head_size)
        blocks = [(i, col) for i in range(u0, u1) for col in cols]
        q = jnp.concatenate([q_all[i, col].reshape(lanes, head_size) for i, col in blocks], 0)
        scores = lax.dot_general(keys, q, (((1,), (1,)), ((), ())), preferred_element_type=jnp.float32)
        key_at = lax.broadcasted_iota(jnp.int32, (UNIT, lanes), 0).astype(jnp.float32) * n
        theirs = [key_at + jnp.concatenate([offs[row, i]] * (lanes // head_size), 1) for i in range(quartet)]
        key_place = jnp.concatenate([x + u * UNIT * n for u in range(u0, u1) for x in theirs], 0)
        weights, shrinks = [], []
        for at, (i, col) in enumerate(blocks):
            s = scores[:, at * lanes : (at + 1) * lanes]
            ours = [jnp.concatenate([offs[z, 2 * col + c]] * (lanes // head_size), 1) for c in range(2)]
            query_place = query_at + i * UNIT * n + jnp.where(first_core, ours[0], ours[1])
            masked = jnp.where(key_place <= query_place, s[below:], -jnp.inf)
            s = jnp.concatenate([s[:below], masked], 0) if below else masked
            top = jnp.max(s, axis=0, keepdims=True)
            if not fresh:
                old = m_ref[i, col]
                top = jnp.maximum(old, top)
                shrink = jnp.exp2((old - top) * factor)
                shrinks.append(shrink)
            w = jnp.exp2((s - top) * factor)
            total = jnp.sum(w, axis=0, keepdims=True)
            m_ref[i, col] = top
            l_ref[i, col] = total if fresh else l_ref[i, col] * shrink + total
            weights.append(w.astype(jnp.bfloat16))
        o = lax.dot_general(
            values, jnp.concatenate(weights, 1), (((0,), (0,)), ((), ())), preferred_element_type=jnp.float32
        )
        for at, (i, col) in enumerate(blocks):
            part = o[:, at * lanes : (at + 1) * lanes]
            acc_ref[i, col] = part if fresh else acc_ref[i, col] * shrinks[at] + part

    def relayed(way, d):
        return reaches(way, 1) & ((d == 1) | (d >= FAR))

    def each(d, do):
        for way in (DOWN, UP):
            row = z + d if way == DOWN else z - d

            @pl.when((row < rows) if way == DOWN else (row >= 0))
            def _():
                do(way, row)

    def relay(d, i):
        def do(way, row):
            @pl.when(relayed(way, d))
            def _():
                if i == 0:
                    mark(way, row).wait_recv()
                    mark(way, row).start()
                for half in (column, other):
                    piece(way, row, i, half).wait_recv()
                    piece(way, row, i, half).start()

        each(d, do)

    def take(d, step):
        def do(way, row):
            @pl.when(jnp.logical_not(relayed(way, d)))
            def _():
                for i in every:
                    if step[0] <= pieces[i][0] < step[1]:
                        if i == 0:
                            mark(way, row).wait_recv()
                        for half in (column, other):
                            piece(way, row, i, half).wait_recv()

            attention((0, 1), row, step)

        each(d, do)

    def finish(i):
        for u in range(*pieces[i]):
            for col in range(2):
                o = acc_ref[u, col] * (1.0 / l_ref[u, col])
                o = o.T.astype(jnp.bfloat16)
                for c in range(2):
                    part = o[c * lanes // 2 : (c + 1) * lanes // 2]
                    o_stage[u, 2 * col + c] = part.reshape(per_group, UNIT, head_size)
        for dst in (across, diagonal, mate):
            back(i, h, dst).start()
        for u in range(*pieces[i]):
            o_all[u, h] = o_stage[u, h]

    near_q(mate, h, 1).wait_recv()
    for step in steps:
        attention([column], z, step, True)
    relay(1, 0)
    relay(1, 1)
    waits(q_all.at[:, other], recv=q_recv.at[0])
    for step in steps:
        attention([other], z, step, True)
        if step[0] == 0:
            for i in every[2:]:
                relay(1, i)

    if rows > FAR + 1:
        for i in every:
            relay(FAR, i)

        @pl.loop(FAR + 1, rows)
        def _(d):
            for i in every:
                relay(d, i)
            for step in steps:
                take(d, step)

    for step in steps:
        for d in (1, 3):
            take(d, step)
    for i in every:
        take(2, pieces[i])
        finish(i)

    for i in every:
        u0, u1 = pieces[i]
        waits(o_all.at[pl.ds(u0, u1 - u0), pl.ds(0, quartet - 1)], recv=o_recv.at[i])
        for u in range(u0, u1):
            for k in range(kv_heads):
                for g in range(per_group):
                    at = u * UNIT * heads + k * per_group + g
                    wide[pl.ds(at, UNIT, stride=heads), :] = o_all[u, k, g].astype(jnp.float32)
        span = slice(u0 * UNIT * heads, u1 * UNIT * heads)
        out_ref[span, :] = wide[span, :].astype(jnp.bfloat16)

    three = pl.ds(0, quartet - 1)
    waits(kv_stage.at[three], send=in_send)
    waits(offs.at[z, three], send=inoff_send)
    waits(q_stage.at[three], send=q_send)
    waits(o_stage.at[:, three], send=o_send)

    def sent(way, row):
        waits(offs.at[row], send=offz_send.at[way, slot(row)])
        waits(kv.at[row], send=z_send.at[way, slot(row)])

    for way in (DOWN, UP):

        @pl.when(reaches(way, 1))
        def _():
            sent(way, z)

        @pl.when(reaches(way, FAR))
        def _():
            waits(offs.at[z], send=far_send.at[2 + way])
            waits(kv.at[z], send=far_send.at[way])

    @pl.loop(1, rows)
    def _(d):
        @pl.when((z + d < rows) & relayed(DOWN, d))
        def _():
            sent(DOWN, z + d)

        @pl.when((z - d >= 0) & relayed(UP, d))
        def _():
            sent(UP, z - d)


def solution(mesh):
    n = mesh.shape["ctx"]

    def shards(queries, keys, values, positions):
        tokens, heads, head_size = queries.shape
        kv_heads = keys.shape[1]
        per_group = heads // kv_heads
        table = rotary_tables(tokens, head_size, n)
        units = tokens // UNIT
        pieces = len(cuts(units)[1])
        rows = n // kv_heads
        lanes = 2 * per_group * UNIT
        vmem = pl.BlockSpec(memory_space=pltpu.VMEM)
        hbm = pl.BlockSpec(memory_space=pl.ANY)
        dma = pltpu.SemaphoreType.DMA
        bf16, f32 = jnp.bfloat16, jnp.float32
        out = pl.pallas_call(
            functools.partial(attend, n, kv_heads, per_group, tokens),
            out_shape=jax.ShapeDtypeStruct((tokens * heads, head_size), bf16),
            in_specs=[hbm] * 5,
            out_specs=vmem,
            scratch_shapes=[
                pltpu.VMEM((rows, units, kv_heads, 2, UNIT, head_size), bf16),
                pltpu.VMEM((kv_heads, units, 2, UNIT, head_size), bf16),
                pltpu.VMEM((units, 2, 2, per_group, UNIT, head_size), bf16),
                pltpu.VMEM((kv_heads, units, per_group, UNIT, head_size), bf16),
                pltpu.VMEM((units, kv_heads, per_group, UNIT, head_size), bf16),
                pltpu.VMEM((units, kv_heads, per_group, UNIT, head_size), bf16),
                pltpu.VMEM((rows, kv_heads, 1, head_size), f32),
                pltpu.VMEM((tokens * heads, head_size), f32),
                pltpu.VMEM((2, tokens * kv_heads, head_size), f32),
                pltpu.VMEM((units, 2, 1, lanes), f32),
                pltpu.VMEM((units, 2, 1, lanes), f32),
                pltpu.VMEM((units, 2, head_size, lanes), f32),
                pltpu.SMEM((tokens,), jnp.int32),
                pltpu.VMEM((tokens * heads, head_size), bf16),
                pltpu.VMEM((tokens * kv_heads, head_size), bf16),
                pltpu.VMEM((tokens * kv_heads, head_size), bf16),
                pltpu.VMEM(table.shape, f32),
                dma((rows, pieces, 2)),
                dma((2, rows - 1)),
                dma((4,)),
                dma((rows,)),
                dma((2, rows - 1)),
                dma((pieces + 1,)),
                dma(()),
                dma((2,)),
                dma(()),
                dma((2,)),
                dma(()),
                dma((pieces,)),
                dma(()),
                pltpu.SemaphoreType.REGULAR,
                dma((5,)),
            ],
            compiler_params=pltpu.CompilerParams(
                collective_id=0, has_side_effects=True, vmem_limit_bytes=48 * 1024 * 1024
            ),
        )(
            *(
                pltpu.with_memory_space_constraint(x, pltpu.HBM)
                for x in (
                    positions,
                    queries.reshape(tokens * heads, head_size),
                    keys.reshape(tokens * kv_heads, head_size),
                    values.reshape(tokens * kv_heads, head_size),
                    jnp.asarray(table),
                )
            )
        )
        return out.reshape(tokens, heads, head_size)

    placed = (
        P(("groups", "ctx"), None, None),
        P(("groups", "ctx"), None, None),
        P(("groups", "ctx"), None, None),
        P(("groups", "ctx")),
    )
    return jax.shard_map(
        shards,
        mesh=mesh,
        in_specs=placed,
        out_specs=P(("groups", "ctx"), None, None),
        check_vma=False,
    )
```

time: 25.9 us -> 24.6 us (0.950)
  Pallas kernels: 25 us -> 23.7 us
    pallas_call x1, Pallas kernels: 25 us -> 23.7 us  [shards(): pl.pallas_call(functools.partial(attend, n, kv_heads, per_group, tokens),...]
where the time goes in v3:
time: 24.6 us; the launch traced here: 24.5 us
  Pallas kernels  23.7 us (96%)
  local copies, waits for them, and re-layouts  0.75 us (3%)
    pallas_call x1, Pallas kernels, shards(): pl.pallas_call(functools.partial(attend, n, kv_heads, per_group, tokens),...  23.7 us
    unnamed x1, local copies, waits for them, and re-layouts  0.75 us

profile of v3, /device:TPU:0, one launch (start us, length us, event | category | flops | bytes accessed | tf_op | source)
XLA Modules:
  0.0 24.5 jit_solution(2964244142899270840)
XLA Ops:
  0.0 23.7 %shard_map.55 = bf16[1536,128]{1,0:T(8,128)(2,1)S(1)} custom-call(s32[96]{0:T(128)} %place_hbm.1, bf16[1536,128]{1,0:T(8,128)(2,1)} %bitcast.5, bf16[384,128]{1,0:T(8,128)(2,1)} %bitcast.6, bf16[384,128]{1,0:T(8,128)(2,1)} %bitcast.7, f32[224,128]{1,0:T(8,128)} %constant.2.clone.table_hbm), custom_call_target="tpu_custom_call" | custom-call | tf_op jit(solution)/shard_map/pallas_call | solution.py:415
  23.7 0.7 %copy.7 = bf16[96,16,128]{2,1,0:T(8,128)(2,1)} copy(bf16[96,16,128]{2,1,0:T(8,128)(2,1)S(1)} %bitcast.4) | data formatting | bytes 786432

commit v4 on v3

--- a/solution.py
+++ b/solution.py
@@ -78,17 +78,13 @@
 
     for peer in (mate, across, diagonal):
         greet(base + peer)
-    greeted = 3 + reaches(DOWN, FAR).astype(jnp.int32)
-    for way in (DOWN, UP):
-        greeted += reaches(way, 1).astype(jnp.int32)
-
-        @pl.when(reaches(way, 1))
-        def _():
-            greet(target(way, 1))
-
-    @pl.when(reaches(UP, FAR))
-    def _():
-        greet(target(UP, FAR))
+    greeted = 3
+    for step in (1, FAR):
+        greeted += reaches(DOWN, step).astype(jnp.int32)
+
+        @pl.when(reaches(UP, step))
+        def _():
+            greet(target(UP, step))
 
     def remote(src, dst, send_sem, recv_sem, target):
         return pltpu.make_async_remote_copy(
@@ -171,26 +167,28 @@
 
     pl.semaphore_wait(barrier, greeted)
 
-    @pl.when(reaches(DOWN, FAR))
-    def _():
-        pl.semaphore_signal(alive, inc=1, device_id={"ctx": target(DOWN, FAR)})
-
-    def spread(which, half, first, count, marks):
-        @pl.when(reaches(DOWN, FAR))
-        def _():
-            if marks:
-                far_mark(DOWN, first, count).start()
-            for i in which:
-                far_piece(DOWN, i, half, first, count).start()
-
-        for way in (DOWN, UP):
-
-            @pl.when(reaches(way, 1))
+    for at, step in enumerate((1, FAR)):
+
+        @pl.when(reaches(DOWN, step))
+        def _():
+            pl.semaphore_signal(alive.at[at], inc=1, device_id={"ctx": target(DOWN, step)})
+
+    def spread(way, which, half, first, count, marks):
+        if way == DOWN:
+
+            @pl.when(reaches(DOWN, FAR))
             def _():
                 if marks:
-                    mark(way, z, first, count).start()
+                    far_mark(DOWN, first, count).start()
                 for i in which:
-                    piece(way, z, i, half, first, count).start()
+                    far_piece(DOWN, i, half, first, count).start()
+
+        @pl.when(reaches(way, 1))
+        def _():
+            if marks:
+                mark(way, z, first, count).start()
+            for i in which:
+                piece(way, z, i, half, first, count).start()
 
     every = range(len(pieces))
     for dst in (across, diagonal):
@@ -200,7 +198,7 @@
             near(i, h, dst).start()
     near_mark(h, mate, 1).start()
     near_whole(h, mate).start()
-    spread(every, column, h, 1, True)
+    spread(DOWN, every, column, h, 1, True)
 
     loads[4].wait()
     wide[...] = q_ref[...].astype(jnp.float32)
@@ -215,18 +213,25 @@
 
     near_mark(mate, h, 1).wait_recv()
     near_whole(mate, h).wait_recv()
-    spread(every, column, mate, 1, True)
+    spread(DOWN, every, column, mate, 1, True)
+
+    @pl.when(reaches(UP, 1))
+    def _():
+        pl.semaphore_wait(alive.at[0], 1)
+
+    spread(UP, every, column, 2 * column, 2, True)
 
     other = 1 - column
     for i in every:
         if i == 0:
             waits(offs.at[z, pl.ds(2 * other, 2)], recv=inoff_recv.at[0])
         waits(part_of(z, i, 2 * other, 2), recv=in_recv.at[i])
-        spread([i], other, 2 * other, 2, i == 0)
+        for way in (DOWN, UP):
+            spread(way, [i], other, 2 * other, 2, i == 0)
 
     @pl.when(reaches(UP, FAR))
     def _():
-        pl.semaphore_wait(alive, 1)
+        pl.semaphore_wait(alive.at[1], 1)
         far_mark(UP).start()
         for i in every:
             for half in (column, other):
@@ -235,24 +240,35 @@
     query_at = (lax.broadcasted_iota(jnp.int32, (1, lanes), 1) % UNIT * n).astype(jnp.float32)
     first_core = lax.broadcasted_iota(jnp.int32, (1, lanes), 1) < lanes // 2
 
-    def attention(cols, row, step, fresh=False):
+    def attention(cols, rows_in, step, span=None, fresh=False):
         u0, u1 = step
-        below, count = u0 * quartet * UNIT, u1 * quartet * UNIT
-        keys = kv[row, :u1, :, 0].reshape(count, head_size)
-        values = kv[row, :u1, :, 1].reshape(count, head_size)
+        k0, k1 = (0, u1) if span is None else span
+        below = max(0, min(u0, k1) - k0) * quartet * UNIT
+        count = (k1 - k0) * quartet * UNIT
+        keys = jnp.concatenate([kv[row, k0:k1, :, 0].reshape(count, head_size) for row in rows_in], 0)
+        values = jnp.concatenate([kv[row, k0:k1, :, 1].reshape(count, head_size) for row in rows_in], 0)
         blocks = [(i, col) for i in range(u0, u1) for col in cols]
         q = jnp.concatenate([q_all[i, col].reshape(lanes, head_size) for i, col in blocks], 0)
         scores = lax.dot_general(keys, q, (((1,), (1,)), ((), ())), preferred_element_type=jnp.float32)
         key_at = lax.broadcasted_iota(jnp.int32, (UNIT, lanes), 0).astype(jnp.float32) * n
-        theirs = [key_at + jnp.concatenate([offs[row, i]] * (lanes // head_size), 1) for i in range(quartet)]
-        key_place = jnp.concatenate([x + u * UNIT * n for u in range(u0, u1) for x in theirs], 0)
+        key_places = []
+        for row in rows_in:
+            theirs = [key_at + jnp.concatenate([offs[row, i]] * (lanes // head_size), 1) for i in range(quartet)]
+            key_places.append(
+                jnp.concatenate([x + u * UNIT * n for u in range(max(u0, k0), k1) for x in theirs], 0)
+            )
         weights, shrinks = [], []
         for at, (i, col) in enumerate(blocks):
             s = scores[:, at * lanes : (at + 1) * lanes]
             ours = [jnp.concatenate([offs[z, 2 * col + c]] * (lanes // head_size), 1) for c in range(2)]
             query_place = query_at + i * UNIT * n + jnp.where(first_core, ours[0], ours[1])
-            masked = jnp.where(key_place <= query_place, s[below:], -jnp.inf)
-            s = jnp.concatenate([s[:below], masked], 0) if below else masked
+            parts = []
+            for r, key_place in enumerate(key_places):
+                if below:
+                    parts.append(s[r * count : r * count + below])
+                late = s[r * count + below : (r + 1) * count]
+                parts.append(jnp.where(key_place <= query_place, late, -jnp.inf))
+            s = jnp.concatenate(parts, 0)
             top = jnp.max(s, axis=0, keepdims=True)
             if not fresh:
                 old = m_ref[i, col]
@@ -295,7 +311,7 @@
 
         each(d, do)
 
-    def take(d, step):
+    def come(d, step):
         def do(way, row):
             @pl.when(jnp.logical_not(relayed(way, d)))
             def _():
@@ -306,9 +322,20 @@
                         for half in (column, other):
                             piece(way, row, i, half).wait_recv()
 
-            attention((0, 1), row, step)
-
         each(d, do)
+
+    def take(d, step, queries=None, span=None):
+        come(d, step)
+        each(d, lambda way, row: attention((0, 1), [row], queries or step, span))
+
+    def take_early(step):
+        if rows == FAR + 1:
+            come(1, step)
+            come(FAR, step)
+            attention((0, 1), [lax.rem(z + 1, rows), lax.rem(z + FAR, rows)], step)
+        else:
+            take(1, step)
+            take(FAR, step)
 
     def finish(i):
         for u in range(*pieces[i]):
@@ -325,15 +352,15 @@
 
     near_q(mate, h, 1).wait_recv()
     for step in steps:
-        attention([column], z, step, True)
+        attention([column], [z], step, fresh=True)
     relay(1, 0)
-    relay(1, 1)
     waits(q_all.at[:, other], recv=q_recv.at[0])
-    for step in steps:
-        attention([other], z, step, True)
-        if step[0] == 0:
-            for i in every[2:]:
-                relay(1, i)
+    for s, step in enumerate(steps):
+        if s == len(steps) - 1:
+            relay(1, 1)
+        attention([other], [z], step, fresh=True)
+    for i in every[2:]:
+        relay(1, i)
 
     if rows > FAR + 1:
         for i in every:
@@ -346,12 +373,18 @@
             for step in steps:
                 take(d, step)
 
-    for step in steps:
-        for d in (1, 3):
-            take(d, step)
-    for i in every:
-        take(2, pieces[i])
-        finish(i)
+    ahead = 0
+    for s, step in enumerate(steps):
+        while ahead < min(s + 2, len(steps)):
+            take_early(steps[ahead])
+            ahead += 1
+        if s < len(steps) - 1:
+            take(2, step)
+            finish(s)
+    take(2, pieces[-2], steps[-1], (0, pieces[-2][1]))
+    finish(len(pieces) - 2)
+    take(2, pieces[-1], pieces[-1], pieces[-1])
+    finish(len(pieces) - 1)
 
     for i in every:
         u0, u1 = pieces[i]
@@ -448,7 +481,7 @@
                 dma(()),
                 dma((pieces,)),
                 dma(()),
-                pltpu.SemaphoreType.REGULAR,
+                pltpu.SemaphoreType.REGULAR((2,)),
                 dma((5,)),
             ],
             compiler_params=pltpu.CompilerParams(

time: 24.6 us -> 24.3 us (0.988)
  Pallas kernels: 23.7 us -> 23.4 us
    pallas_call x1, Pallas kernels: 23.7 us -> 23.4 us  [shards(): pl.pallas_call(functools.partial(attend, n, kv_heads, per_group, tokens),...]
where the time goes in v4:
time: 24.3 us; the launch traced here: 24.1 us
  Pallas kernels  23.4 us (96%)
  local copies, waits for them, and re-layouts  0.75 us (3%)
    pallas_call x1, Pallas kernels, shards(): pl.pallas_call(functools.partial(attend, n, kv_heads, per_group, tokens),...  23.4 us
    unnamed x1, local copies, waits for them, and re-layouts  0.75 us

profile of v4, /device:TPU:0, one launch (start us, length us, event | category | flops | bytes accessed | tf_op | source)
XLA Modules:
  0.0 24.1 jit_solution(13256848358805596229)
XLA Ops:
  0.0 23.4 %shard_map.55 = bf16[1536,128]{1,0:T(8,128)(2,1)S(1)} custom-call(s32[96]{0:T(128)} %place_hbm.1, bf16[1536,128]{1,0:T(8,128)(2,1)} %bitcast.5, bf16[384,128]{1,0:T(8,128)(2,1)} %bitcast.6, bf16[384,128]{1,0:T(8,128)(2,1)} %bitcast.7, f32[224,128]{1,0:T(8,128)} %constant.2.clone.table_hbm), custom_call_target="tpu_custom_call" | custom-call | tf_op jit(solution)/shard_map/pallas_call | solution.py:448
  23.4 0.7 %copy.7 = bf16[96,16,128]{2,1,0:T(8,128)(2,1)} copy(bf16[96,16,128]{2,1,0:T(8,128)(2,1)S(1)} %bitcast.4) | data formatting | bytes 786432

commit v5 on v4

--- a/solution.py
+++ b/solution.py
@@ -10,6 +10,7 @@
 from jax.sharding import PartitionSpec as P
 
 UNIT = 16
+CHUNKS = 3
 DOWN, UP = 0, 1
 FAR = 3
 
@@ -45,8 +46,12 @@
             [(place_hbm, place_ref), (table_hbm, table_ref), (k_hbm, k_ref), (v_hbm, v_ref), (q_hbm, q_ref)]
         )
     ]
-    for load in loads:
-        load.start()
+    for at, src, dst in ((2, k_hbm, k_ref), (3, v_hbm, v_ref), (1, table_hbm, table_ref)):
+        size = src.shape[0] // CHUNKS // 8 * 8
+        for c in range(CHUNKS):
+            span = pl.ds(c * size, size if c < CHUNKS - 1 else src.shape[0] - c * size)
+            pltpu.make_async_copy(src.at[span], dst.at[span], load_sem.at[at]).start()
+    loads[0].start()
     head_size = q_ref.shape[-1]
     heads = kv_heads * per_group
     quartet = kv_heads
@@ -91,29 +96,47 @@
             src_ref=src, dst_ref=dst, send_sem=send_sem, recv_sem=recv_sem, device_id={"ctx": target}
         )
 
-    def part_of(row, i, first, count):
-        u0, u1 = pieces[i]
+    mine = [(pieces[0], 0), ((pieces[0][1], units), 1)]
+    others = [(span, 2 + i) for i, span in enumerate(pieces)]
+
+    def part_of(row, item, first, count):
+        (u0, u1), _ = item
         return kv.at[row, pl.ds(u0, u1 - u0), pl.ds(first, count)]
 
     def slot(row):
         d = jnp.abs(row - z)
         return jnp.where(d > 1, d - 1, d)
 
-    def piece(way, row, i, half, first=None, count=2):
-        part = part_of(row, i, 2 * half if first is None else first, count)
-        return remote(part, part, z_send.at[way, slot(row)], kv_recv.at[row, i, half], target(way, 1))
-
-    def far_piece(way, i, half, first=None, count=2):
-        part = part_of(z, i, 2 * half if first is None else first, count)
-        return remote(part, part, far_send.at[way], kv_recv.at[z, i, half], target(way, FAR))
+    def inbox(row, item, place):
+        return kv_recv.at[lax.rem(row - place + rows, rows) - 1, item[1]]
+
+    def mailbox(row, place):
+        return off_recv.at[lax.rem(row - place + rows, rows) - 1]
+
+    def reached(way, step):
+        return z - step if way == DOWN else z + step
+
+    def piece(way, row, item, half, first=None, count=2):
+        part = part_of(row, item, 2 * half if first is None else first, count)
+        return remote(part, part, z_send.at[way, slot(row)], inbox(row, item, reached(way, 1)), target(way, 1))
 
     def mark(way, row, first=0, count=quartet):
         part = offs.at[row, pl.ds(first, count)]
-        return remote(part, part, offz_send.at[way, slot(row)], off_recv.at[row], target(way, 1))
-
-    def far_mark(way, first=0, count=quartet):
+        return remote(part, part, offz_send.at[way, slot(row)], mailbox(row, reached(way, 1)), target(way, 1))
+
+    def straight(way, item, half, first=None, count=2):
+        part = part_of(z, item, 2 * half if first is None else first, count)
+        return remote(part, part, far_send.at[way], inbox(z, item, reached(way, FAR)), target(way, FAR))
+
+    def straight_mark(way, first=0, count=quartet):
         part = offs.at[z, pl.ds(first, count)]
-        return remote(part, part, far_send.at[2 + way], off_recv.at[z], target(way, FAR))
+        return remote(part, part, far_send.at[2 + way], mailbox(z, reached(way, FAR)), target(way, FAR))
+
+    def got(row, item, half):
+        waits(part_of(row, item, 2 * half, 2), recv=inbox(row, item, z))
+
+    def got_mark(row):
+        waits(offs.at[row], recv=mailbox(row, z))
 
     def near(i, src, dst):
         u0, u1 = pieces[i]
@@ -156,6 +179,7 @@
     offs[z, h] = jnp.full((1, head_size), offset.astype(jnp.float32), jnp.float32)
     for load in loads[2:4]:
         load.wait()
+    loads[4].start()
     small[0] = k_ref[...].astype(jnp.float32)
     small[1] = v_ref[...].astype(jnp.float32)
     for k in range(kv_heads):
@@ -173,22 +197,22 @@
         def _():
             pl.semaphore_signal(alive.at[at], inc=1, device_id={"ctx": target(DOWN, step)})
 
-    def spread(way, which, half, first, count, marks):
+    def spread(way, items, half, first, count, marks):
         if way == DOWN:
 
             @pl.when(reaches(DOWN, FAR))
             def _():
                 if marks:
-                    far_mark(DOWN, first, count).start()
-                for i in which:
-                    far_piece(DOWN, i, half, first, count).start()
+                    straight_mark(DOWN, first, count).start()
+                for item in items:
+                    straight(DOWN, item, half, first, count).start()
 
         @pl.when(reaches(way, 1))
         def _():
             if marks:
                 mark(way, z, first, count).start()
-            for i in which:
-                piece(way, z, i, half, first, count).start()
+            for item in items:
+                piece(way, z, item, half, first, count).start()
 
     every = range(len(pieces))
     for dst in (across, diagonal):
@@ -198,7 +222,7 @@
             near(i, h, dst).start()
     near_mark(h, mate, 1).start()
     near_whole(h, mate).start()
-    spread(DOWN, every, column, h, 1, True)
+    spread(DOWN, mine, column, h, 1, True)
 
     loads[4].wait()
     wide[...] = q_ref[...].astype(jnp.float32)
@@ -213,29 +237,29 @@
 
     near_mark(mate, h, 1).wait_recv()
     near_whole(mate, h).wait_recv()
-    spread(DOWN, every, column, mate, 1, True)
+    spread(DOWN, mine, column, mate, 1, True)
 
     @pl.when(reaches(UP, 1))
     def _():
         pl.semaphore_wait(alive.at[0], 1)
 
-    spread(UP, every, column, 2 * column, 2, True)
+    spread(UP, mine, column, 2 * column, 2, True)
 
     other = 1 - column
     for i in every:
         if i == 0:
             waits(offs.at[z, pl.ds(2 * other, 2)], recv=inoff_recv.at[0])
-        waits(part_of(z, i, 2 * other, 2), recv=in_recv.at[i])
+        waits(part_of(z, others[i], 2 * other, 2), recv=in_recv.at[i])
         for way in (DOWN, UP):
-            spread(way, [i], other, 2 * other, 2, i == 0)
+            spread(way, [others[i]], other, 2 * other, 2, i == 0)
 
     @pl.when(reaches(UP, FAR))
     def _():
         pl.semaphore_wait(alive.at[1], 1)
-        far_mark(UP).start()
-        for i in every:
-            for half in (column, other):
-                far_piece(UP, i, half).start()
+        straight_mark(UP).start()
+        for items, half in ((mine, column), (others, other)):
+            for item in items:
+                straight(UP, item, half).start()
 
     query_at = (lax.broadcasted_iota(jnp.int32, (1, lanes), 1) % UNIT * n).astype(jnp.float32)
     first_core = lax.broadcasted_iota(jnp.int32, (1, lanes), 1) < lanes // 2
@@ -298,16 +322,19 @@
             def _():
                 do(way, row)
 
+    def halves(i):
+        return [(items[i], half) for items, half in ((mine, column), (others, other)) if i < len(items)]
+
     def relay(d, i):
         def do(way, row):
             @pl.when(relayed(way, d))
             def _():
                 if i == 0:
-                    mark(way, row).wait_recv()
+                    got_mark(row)
                     mark(way, row).start()
-                for half in (column, other):
-                    piece(way, row, i, half).wait_recv()
-                    piece(way, row, i, half).start()
+                for item, half in halves(i):
+                    got(row, item, half)
+                    piece(way, row, item, half).start()
 
         each(d, do)
 
@@ -318,9 +345,9 @@
                 for i in every:
                     if step[0] <= pieces[i][0] < step[1]:
                         if i == 0:
-                            mark(way, row).wait_recv()
-                        for half in (column, other):
-                            piece(way, row, i, half).wait_recv()
+                            got_mark(row)
+                        for item, half in halves(i):
+                            got(row, item, half)
 
         each(d, do)
 
@@ -386,6 +413,36 @@
     take(2, pieces[-1], pieces[-1], pieces[-1])
     finish(len(pieces) - 1)
 
+    three = pl.ds(0, quartet - 1)
+    waits(kv_stage.at[three], send=in_send)
+    waits(offs.at[z, three], send=inoff_send)
+    waits(q_stage.at[three], send=q_send)
+
+    def sent(way, row):
+        waits(offs.at[row], send=offz_send.at[way, slot(row)])
+        waits(kv.at[row], send=z_send.at[way, slot(row)])
+
+    for way in (DOWN, UP):
+
+        @pl.when(reaches(way, 1))
+        def _():
+            sent(way, z)
+
+        @pl.when(reaches(way, FAR))
+        def _():
+            waits(offs.at[z], send=far_send.at[2 + way])
+            waits(kv.at[z], send=far_send.at[way])
+
+    @pl.loop(1, rows)
+    def _(d):
+        @pl.when((z + d < rows) & relayed(DOWN, d))
+        def _():
+            sent(DOWN, z + d)
+
+        @pl.when((z - d >= 0) & relayed(UP, d))
+        def _():
+            sent(UP, z - d)
+
     for i in every:
         u0, u1 = pieces[i]
         waits(o_all.at[pl.ds(u0, u1 - u0), pl.ds(0, quartet - 1)], recv=o_recv.at[i])
@@ -397,36 +454,7 @@
         span = slice(u0 * UNIT * heads, u1 * UNIT * heads)
         out_ref[span, :] = wide[span, :].astype(jnp.bfloat16)
 
-    three = pl.ds(0, quartet - 1)
-    waits(kv_stage.at[three], send=in_send)
-    waits(offs.at[z, three], send=inoff_send)
-    waits(q_stage.at[three], send=q_send)
-    waits(o_stage.at[:, three], send=o_send)
-
-    def sent(way, row):
-        waits(offs.at[row], send=offz_send.at[way, slot(row)])
-        waits(kv.at[row], send=z_send.at[way, slot(row)])
-
-    for way in (DOWN, UP):
-
-        @pl.when(reaches(way, 1))
-        def _():
-            sent(way, z)
-
-        @pl.when(reaches(way, FAR))
-        def _():
-            waits(offs.at[z], send=far_send.at[2 + way])
-            waits(kv.at[z], send=far_send.at[way])
-
-    @pl.loop(1, rows)
-    def _(d):
-        @pl.when((z + d < rows) & relayed(DOWN, d))
-        def _():
-            sent(DOWN, z + d)
-
-        @pl.when((z - d >= 0) & relayed(UP, d))
-        def _():
-            sent(UP, z - d)
+    waits(o_stage.at[:, pl.ds(0, quartet - 1)], send=o_send)
 
 
 def solution(mesh):
@@ -468,11 +496,11 @@
                 pltpu.VMEM((tokens * kv_heads, head_size), bf16),
                 pltpu.VMEM((tokens * kv_heads, head_size), bf16),
                 pltpu.VMEM(table.shape, f32),
-                dma((rows, pieces, 2)),
-                dma((2, rows - 1)),
+                dma((rows - 1, pieces + 2)),
+                dma((2, max(2, rows - 2))),
                 dma((4,)),
-                dma((rows,)),
-                dma((2, rows - 1)),
+                dma((rows - 1,)),
+                dma((2, max(2, rows - 2))),
                 dma((pieces + 1,)),
                 dma(()),
                 dma((2,)),

time: 24.3 us -> 24.3 us (level)
  no operation moved by 1% of the time
where the time goes in v5:
time: 24.3 us; the launch traced here: 24.2 us
  Pallas kernels  23.4 us (96%)
  local copies, waits for them, and re-layouts  0.75 us (3%)
    pallas_call x1, Pallas kernels, shards(): pl.pallas_call(functools.partial(attend, n, kv_heads, per_group, tokens),...  23.4 us
    unnamed x1, local copies, waits for them, and re-layouts  0.75 us

profile of v5, /device:TPU:0, one launch (start us, length us, event | category | flops | bytes accessed | tf_op | source)
XLA Modules:
  0.0 24.2 jit_solution(8942820103850042274)
XLA Ops:
  0.0 23.4 %shard_map.55 = bf16[1536,128]{1,0:T(8,128)(2,1)S(1)} custom-call(s32[96]{0:T(128)} %place_hbm.1, bf16[1536,128]{1,0:T(8,128)(2,1)} %bitcast.5, bf16[384,128]{1,0:T(8,128)(2,1)} %bitcast.6, bf16[384,128]{1,0:T(8,128)(2,1)} %bitcast.7, f32[224,128]{1,0:T(8,128)} %constant.2.clone.table_hbm), custom_call_target="tpu_custom_call" | custom-call | tf_op jit(solution)/shard_map/pallas_call | solution.py:476
  23.4 0.7 %copy.7 = bf16[96,16,128]{2,1,0:T(8,128)(2,1)} copy(bf16[96,16,128]{2,1,0:T(8,128)(2,1)S(1)} %bitcast.4) | data formatting | bytes 786432
